TPU v7x, 32 devices: a 4x4x1 block of a 4x4x8 slice. The times are simulated.
32 devices in a mesh: kv: 1 (over z), dup: 32 (over y, x, core).
Axes of the slice: x: 4, y: 4, z: 1, core: 2. Of those that a mesh axis runs over, the one named last changes fastest.
The devices are a block of a 4x4x8 slice.
Arguments:
- queries: bfloat16 [256, 64, 128], P('kv', 'dup')
- key_cache: bfloat16 [256, 4096, 128], P('kv', 'dup')
- value_cache: bfloat16 [256, 4096, 128], P('kv', 'dup')
- lengths: int32 [256], P('kv')
Outputs:
- output: bfloat16 [256, 64, 128], P('kv', 'dup')
All inputs are finite; a program needn't handle non-finite values.
Results may differ from a plain program's by a relative error of at most 0.00787467.
Values are sent between devices in bfloat16 or wider.
A program may use at most 768 MiB of HBM per device.

v0:
```python
import jax
import jax.numpy as jnp
from jax import lax
from jax.sharding import PartitionSpec as P, NamedSharding

DRAFT = 4
NEG_BIG = -1e30


def solution(mesh):
    dup_size = mesh.shape["dup"]

    def group_step(q_local, k_span, v_span, len_local):
        num_batch, span_len, head_dim = k_span.shape
        span_start = lax.axis_index("dup") * span_len
        q_group = lax.all_gather(q_local, "dup", axis=1, tiled=True)
        num_rows = q_group.shape[1]
        own_rows = num_rows // dup_size
        scores = jnp.einsum("brd,bsd->brs", q_group, k_span, preferred_element_type=jnp.float32) * (head_dim ** -0.5)
        last_pos = len_local[:, None] - DRAFT + (jnp.arange(num_rows) % DRAFT)[None, :]
        allowed = (span_start + jnp.arange(span_len))[None, None, :] <= last_pos[:, :, None]
        scores = jnp.where(allowed, scores, NEG_BIG)
        row_peak = jnp.max(scores, axis=2, keepdims=True)
        prob_vals = jnp.exp(scores - row_peak)
        row_mass = jnp.sum(prob_vals, axis=2, keepdims=True)
        weighted = jnp.einsum("brs,bsd->brd", prob_vals.astype(jnp.bfloat16), v_span, preferred_element_type=jnp.float32)
        part_out = (weighted / row_mass).astype(jnp.bfloat16).reshape(num_batch, dup_size, own_rows, head_dim)
        log_mass = (row_peak + jnp.log(row_mass)).reshape(num_batch, dup_size, own_rows)
        recv_out = lax.all_to_all(part_out, "dup", 1, 1)
        recv_mass = lax.all_to_all(log_mass, "dup", 1, 1)
        top_mass = jnp.max(recv_mass, axis=1, keepdims=True)
        weights = jnp.exp(recv_mass - top_mass)
        total_mass = jnp.sum(weights, axis=1)
        merged = jnp.sum(weights[..., None] * recv_out.astype(jnp.float32), axis=1)
        return (merged / total_mass[..., None]).astype(jnp.bfloat16)

    return jax.shard_map(group_step, mesh=mesh, in_specs=(P("kv", "dup", None), P("kv", "dup", None), P("kv", "dup", None), P("kv")), out_specs=P("kv", "dup", None), check_vma=False)
```

profile of v0, /device:TPU:96, one launch (start us, length us, event | category | flops | bytes accessed | tf_op | source)
XLA Modules:
  0.0 179.4 jit_solution(18045567292857291077)
XLA Ops:
  6.5 0.0 all-gather.2.cloned.1.call-start
  6.6 1.6 copy.8
  8.1 0.1 all-gather.2.cloned.1.call-update
  8.2 0.7 broadcast_add_fusion.1
  8.9 0.1 broadcast_add_fusion
  9.0 43.9 %all-gather.2.cloned.1.call-done = bf16[256,64,128]{2,0,1:T(8,128)(2,1)} async-done(((bf16[256,2,128]{2,0,1:T(8,128)(2,1)}), bf16[256,64,128]{2,0,1:T(8,128)(2,1)}) %all-gather.2.cloned.1.call-update) | async-done | bytes 4194320 | tf_op jit(solution)/shard_map/all_gather | solution.py:16
  52.9 10.3 %fusion.2 = (f32[256,64]{1,0:T(8,128)S(1)}, f32[256,64,128]{2,1,0:T(8,128)S(1)}) fusion(s32[256,64]{1,0:T(8,128)S(1)} %broadcast_add_fusion, s32[128]{0:T(128)S(1)} %iota_add_fusion, bf16[256,128,128]{2,1,0:T(8,128)(2,1)} %param.5, bf16[256,64,128]{2,0,1:T(8,128)(2,1)} %all-gather.2.cloned.1.call-done), kind=kOutput, calls=%fused_computation.6 | convolution fusion | flops 545243136 | bytes 21103104 | tf_op jit(solution)/shard_map/brd,bsd->brs/dot_general | solution.py:19
  63.2 0.0 copy-start
  63.2 3.2 %copy-done = f32[256,64,128]{2,1,0:T(8,128)} copy-done((f32[256,64,128]{2,1,0:T(8,128)}, f32[256,64,128]{2,1,0:T(8,128)S(1)}, u32[]{:S(2)}) %copy-start) | copy-done | bytes 8388632
  66.4 8.4 %fusion.1 = f32[256,64]{1,0:T(8,128)S(1)} fusion(f32[256,64,128]{2,1,0:T(8,128)S(1)} %get-tuple-element.8, f32[256,64]{1,0:T(8,128)S(1)} %get-tuple-element.7, s32[256,64]{1,0:T(8,128)S(1)} %broadcast_add_fusion, s32[128]{0:T(128)S(1)} %iota_add_fusion), kind=kLoop, calls=%fused_computation.5 | loop fusion | flops 10469376 | bytes 8585728 | tf_op jit(solution)/shard_map/reduce_sum | solution.py:25
  74.8 0.1 copy.10
  74.9 0.7 add.55
  75.6 4.7 %all-to-all-start = ((f32[256,32,2]{0,2,1:T(2,128)}), f32[256,32,2]{0,2,1:T(2,128)S(1)}, u32[]{:S(2)}, u32[]{:S(2)}) async-start(f32[256,32,2]{0,2,1:T(2,128)} %add.55), calls=%async_computation | async-start | bytes 131072 | tf_op jit(solution)/shard_map/all_to_all | solution.py:30
  80.2 11.1 %divide_convert_fusion = bf16[256,64,128]{2,1,0:T(8,128)(2,1)S(1)} fusion(f32[256,64]{1,0:T(8,128)S(1)} %fusion.1, bf16[256,128,128]{2,1,0:T(8,128)(2,1)} %param.6, f32[256,64,128]{2,1,0:T(8,128)} %copy-done, f32[256,64]{1,0:T(8,128)S(1)} %get-tuple-element.7, s32[256,64]{1,0:T(8,128)S(1)} %broadcast_add_fusion, s32[128]{0:T(128)S(1)} %iota_add_fusion), kind=kOutput, calls=%fused_computation.1 | convolution fusion | flops 551550976 | bytes 21168640 | tf_op jit(solution)/shard_map/brs,bsd->brd/dot_general | solution.py:26
  91.4 6.4 %copy.12 = bf16[256,32,2,128]{3,2,0,1:T(2,128)(2,1)} copy(bf16[256,32,2,128]{3,2,1,0:T(2,128)(2,1)S(1)} %bitcast.5) | data formatting | bytes 8388608 | tf_op jit(solution)/shard_map/reshape | solution.py:27
  97.8 0.0 all-to-all-done
  97.8 6.3 %all-to-all-start.1 = ((bf16[256,32,2,128]{3,2,0,1:T(2,128)(2,1)}), bf16[256,32,2,128]{3,2,0,1:T(2,128)(2,1)}, u32[]{:S(2)}, u32[]{:S(2)}) async-start(bf16[256,32,2,128]{3,2,0,1:T(2,128)(2,1)} %copy.12), calls=%async_computation.1 | async-start | bytes 8388608 | tf_op jit(solution)/shard_map/all_to_all | solution.py:29
  104.2 0.1 fusion.16
  104.2 0.1 copy.13
  104.4 2.6 %copy.11 = f32[256,32,2]{2,0,1:T(8,128)} copy(f32[256,32,2]{0,2,1:T(2,128)S(1)} %get-tuple-element.6) | data formatting | bytes 131072 | tf_op jit(solution)/shard_map/exp | solution.py:32
  107.0 53.0 %all-to-all-done.1 = bf16[256,32,2,128]{3,2,0,1:T(2,128)(2,1)} async-done(((bf16[256,32,2,128]{3,2,0,1:T(2,128)(2,1)}), bf16[256,32,2,128]{3,2,0,1:T(2,128)(2,1)}, u32[]{:S(2)}, u32[]{:S(2)}) %all-to-all-start.1) | async-done | bytes 4194336 | tf_op jit(solution)/shard_map/all_to_all | solution.py:29
  160.0 11.5 %multiply_reduce_fusion = f32[256,2,128]{2,1,0:T(2,128)S(1)} fusion(bf16[256,32,2,128]{3,2,0,1:T(2,128)(2,1)} %all-to-all-done.1, f32[256,32,2]{2,0,1:T(8,128)} %copy.11), kind=kLoop, calls=%fused_computation | loop fusion | flops 6225920 | bytes 4521984 | tf_op jit(solution)/shard_map/reduce_sum | solution.py:34
  171.6 1.0 divide_convert_fusion.1
  (4 shorter events, 0.1 us)
Async XLA Ops:
  6.5 46.3 %all-gather.2.cloned.1.call-start = ((), (), s32[]{:S(2)}) async-start(), calls=%async_computation.2 | async-start | bytes 4325376 | tf_op jit(solution)/shard_map/all_gather | solution.py:16
  63.2 3.2 %copy-start = (f32[256,64,128]{2,1,0:T(8,128)}, f32[256,64,128]{2,1,0:T(8,128)S(1)}, u32[]{:S(2)}) copy-start(f32[256,64,128]{2,1,0:T(8,128)S(1)} %get-tuple-element.8) | copy-start | bytes 25165828
  75.6 22.2 %all-to-all-start = ((f32[256,32,2]{0,2,1:T(2,128)}), f32[256,32,2]{0,2,1:T(2,128)S(1)}, u32[]{:S(2)}, u32[]{:S(2)}) async-start(f32[256,32,2]{0,2,1:T(2,128)} %add.55), calls=%async_computation | async-start | bytes 131072 | tf_op jit(solution)/shard_map/all_to_all | solution.py:30
  97.8 62.2 %all-to-all-start.1 = ((bf16[256,32,2,128]{3,2,0,1:T(2,128)(2,1)}), bf16[256,32,2,128]{3,2,0,1:T(2,128)(2,1)}, u32[]{:S(2)}, u32[]{:S(2)}) async-start(bf16[256,32,2,128]{3,2,0,1:T(2,128)(2,1)} %copy.12), calls=%async_computation.1 | async-start | bytes 8388608 | tf_op jit(solution)/shard_map/all_to_all | solution.py:29
Sparse Core Ops, SparseCore 0:
  9.4 43.3 all-gather.1
where the time goes:
time: 181 us; the launch traced here: 179 us
  waiting for transfers between devices  96.9 us (54%)
  other arithmetic  21.8 us (12%)
  matrix products  21.4 us (12%)
  local copies, waits for them, and re-layouts  14.7 us (8%)
  between operations  13.5 us (7%)
  starting transfers between devices  11 us (6%)
    all_to_all x1, waiting for transfers between devices, group_step(): recv_out = lax.all_to_all(part_out, 'dup', 1, 1)  53 us
    all_gather x1, waiting for transfers between devices, group_step(): q_group = lax.all_gather(q_local, 'dup', axis=1, tiled=True)  43.9 us
    reduce_sum x1, other arithmetic, group_step(): merged = jnp.sum(weights[..., None] * recv_out.astype(jnp.float32), axis=1)  11.5 us
    dot_general x1, matrix products, group_step(): jnp.einsum('brs,bsd->brd', prob_vals.astype(jnp.bfloat16), v_span, prefer...  11.1 us
    dot_general x1, matrix products, group_step(): jnp.einsum('brd,bsd->brs', q_group, k_span, preferred_element_type=jnp.fl...  10.3 us
    reduce_sum x1, other arithmetic, group_step(): row_mass = jnp.sum(prob_vals, axis=2, keepdims=True)  8.39 us
    reshape x1, local copies, waits for them, and re-layouts, group_step(): (weighted / row_mass).astype(jnp.bfloat16)  6.42 us
    all_to_all x1, starting transfers between devices, group_step(): recv_out = lax.all_to_all(part_out, 'dup', 1, 1)  6.33 us
  transfers between devices with their start and end apart: 3, of which 2 were waited for; matrix products, arithmetic and copies ran while one was open for 12% of the time, Pallas kernels for 0%

commit v1 on v0

v1 whole, which is shorter than its diff:
```python
import functools
import math

import jax
import jax.numpy as jnp
from jax import lax
from jax.experimental import pallas as pl
from jax.experimental.pallas import tpu as pltpu
from jax.sharding import PartitionSpec as P

DRAFT = 4
CORES = 2
LANES = 128
TILE = 16
MASKED = -3.0e38
MESH = pl.DeviceIdType.MESH
F32 = jnp.float32
BF16 = jnp.bfloat16


def mixing(lams):
    top = functools.reduce(jnp.maximum, lams)
    parts = [jnp.exp2(lam - top) for lam in lams]
    total = functools.reduce(jnp.add, parts)
    inv = 1.0 / total
    return [part * inv for part in parts], top + jnp.log2(total)


def kernel(side, chunks, span, q_hbm, k_hbm, v_hbm, len_ref, out_ref,
           k_buf, v_buf, q_buf, o_buf, wt_buf,
           s0_o, s0_l, r0_o, r0_l, own_l,
           m0_o, m0_l, rel_o, rel_l, com_o, com_l, frm_o, frm_l,
           m1_o, m1_l, r1_o, r1_l,
           in_sem, ag1_s, ag1_r, ag2_s, ag2_r, agc_s, agc_r,
           rsc_s, rsc_r, rs2_s, rs2_r, rs1_s, rs1_r):
    seqs = q_buf.shape[1]
    rows = q_buf.shape[2] * q_buf.shape[3] * q_buf.shape[4] * q_buf.shape[5]
    own = q_buf.shape[5]
    head_dim = q_buf.shape[6]
    half_rows = rows // CORES
    pitch = o_buf.shape[1] // rows
    line = side * own
    hrow = line // 2

    me = lax.axis_index("dup")
    core = lax.rem(me, CORES)
    chip = me // CORES
    x, y = lax.rem(chip, side), chip // side
    a1 = x * (1 - core) + y * core
    a2 = y * (1 - core) + x * core
    step1 = (1 - core) + side * core
    step2 = side * (1 - core) + core

    def device(i1, i2):
        return (i1 * step1 + i2 * step2) * CORES + core

    def wrap(i):
        return lax.rem(i + side, side)

    twin = me + 1 - 2 * core
    right = device(a1, wrap(a2 + 1))
    left = device(a1, wrap(a2 - 1))
    peers = [device(wrap(a1 + d), a2) for d in range(1, side)]

    def send(src, dst, ssem, rsem, to):
        copy = pltpu.make_async_remote_copy(
            src_ref=src, dst_ref=dst, send_sem=ssem, recv_sem=rsem, device_id={"dup": to}, device_id_type=MESH)
        copy.start()
        return copy

    q_in = [pltpu.make_async_copy(q_hbm.at[pl.ds(k * seqs, seqs)], q_buf.at[k, :, 0, a2, a1], in_sem.at[0, k])
            for k in range(chunks)]
    kv_in = []
    for k in range(chunks):
        part = pl.ds(k * seqs, seqs)
        kv_in.append((pltpu.make_async_copy(k_hbm.at[part], k_buf.at[part], in_sem.at[1, k]),
                      pltpu.make_async_copy(v_hbm.at[part], v_buf.at[part], in_sem.at[2, k])))
    for copy in q_in:
        copy.start()
    for pair in kv_in:
        pair[0].start()
        pair[1].start()

    barrier = pltpu.get_barrier_semaphore()
    talk = [twin, right, left] + peers
    for dev in talk:
        pl.semaphore_signal(barrier, inc=1, device_id={"dup": dev}, device_id_type=MESH)
    pl.semaphore_wait(barrier, len(talk))

    sent = []
    got = {}

    def push(key, *args):
        copy = send(*args)
        sent.append(copy)
        got[key] = copy

    def gather1(k):
        q_in[k].wait()
        mine = q_buf.at[k, :, 0, a2, a1]
        for i, dev in enumerate(peers):
            push(("g1", k, i), mine, mine, ag1_s.at[k, i], ag1_r.at[k, i], dev)

    def gather2(k):
        for i in range(side - 1):
            got["g1", k, i].wait_recv()
        mine = q_buf.at[k, :, 0, a2]
        push(("g2", k, 0), mine, mine, ag2_s.at[k, 0], ag2_r.at[k, 0], right)
        push(("g2", k, 1), mine, mine, ag2_s.at[k, 1], ag2_r.at[k, 1], left)
        push(("gc", k, 0), mine, q_buf.at[k, :, 1, a2], agc_s.at[k, 0], agc_r.at[k, 0], twin)

    def gather3(k):
        mid = seqs // 2
        from_left, from_right = wrap(a2 - 1), wrap(a2 + 1)
        got["g2", k, 0].wait_recv()
        lo = q_buf.at[k, pl.ds(0, mid), 0, from_left]
        push(("g2", k, 2), lo, lo, ag2_s.at[k, 2], ag2_r.at[k, 2], right)
        push(("gc", k, 1), q_buf.at[k, :, 0, from_left], q_buf.at[k, :, 1, from_left],
             agc_s.at[k, 1], agc_r.at[k, 1], twin)
        got["g2", k, 1].wait_recv()
        hi = q_buf.at[k, pl.ds(mid, mid), 0, from_right]
        push(("g2", k, 3), hi, hi, ag2_s.at[k, 3], ag2_r.at[k, 3], left)
        push(("gc", k, 2), q_buf.at[k, :, 0, from_right], q_buf.at[k, :, 1, from_right],
             agc_s.at[k, 2], agc_r.at[k, 2], twin)

    def gather4(k):
        got["g2", k, 2].wait_recv()
        got["g2", k, 3].wait_recv()
        far = wrap(a2 + 2)
        push(("gc", k, 3), q_buf.at[k, :, 0, far], q_buf.at[k, :, 1, far], agc_s.at[k, 3], agc_r.at[k, 3], twin)

    def gather5(k):
        for i in range(side):
            got["gc", k, i].wait_recv()

    scale = (head_dim ** -0.5) * math.log2(math.e)

    def attend(k):
        kv_in[k][0].wait()
        kv_in[k][1].wait()
        row = lax.broadcasted_iota(jnp.int32, (rows, span), 0)
        lane = lax.broadcasted_iota(jnp.int32, (rows, span), 1)
        token = jnp.where(row < half_rows, core, 1 - core) * own + jnp.bitwise_and(row, own - 1)
        ahead = lane - token
        first = DRAFT + me * span
        seq_lane = lax.broadcasted_iota(jnp.int32, (rows, LANES), 1)
        slot = k % 2

        def step(b, lam):
            query = q_buf[k, b].reshape(rows, head_dim)
            s = lax.dot_general(query, k_buf[k * seqs + b], (((1,), (1,)), ((), ())), preferred_element_type=F32)
            s = jnp.where(ahead <= len_ref[k * seqs + b] - first, s, MASKED)
            top = jnp.max(s, axis=1, keepdims=True)
            p = jnp.exp2((s - top) * scale)
            mass = jnp.sum(p, axis=1, keepdims=True)
            o = jnp.dot(p.astype(BF16), v_buf[k * seqs + b], preferred_element_type=F32)
            o_buf[slot, pl.ds(b, rows, stride=pitch), :] = o * (1.0 / mass)
            return jnp.where(seq_lane == b, top * scale + jnp.log2(mass), lam)

        lam = lax.fori_loop(0, seqs, step, jnp.zeros((rows, LANES), F32), unroll=4)
        own_l[k] = lam[:half_rows]
        s0_l[k] = lam[half_rows:]

        def pack(t, carry):
            base = pl.multiple_of(t * TILE, TILE)
            for r in range(half_rows):
                s0_o[k, r, pl.ds(base, TILE), :] = o_buf[slot, pl.ds((half_rows + r) * pitch + base, TILE), :].astype(BF16)
            return carry

        lax.fori_loop(0, seqs // TILE, pack, 0)
        push(("c_l", k), s0_l.at[k], r0_l.at[k], rsc_s.at[k, 1], rsc_r.at[k, 1], twin)
        push(("c_o", k), s0_o.at[k], r0_o.at[k], rsc_s.at[k, 0], rsc_r.at[k, 0], twin)

    def turn(weights):
        stack = jnp.concatenate(weights, axis=0)
        if stack.shape[0] < LANES:
            stack = jnp.concatenate([stack, jnp.zeros((LANES - stack.shape[0], LANES), F32)], axis=0)
        wt_buf[...] = stack.T

    def blend(count, parts, store):
        def body(t, carry):
            base = pl.multiple_of(t * TILE, TILE)
            wt = wt_buf[pl.ds(base, TILE), :]
            for r in range(count):
                acc = None
                for i, part in enumerate(parts):
                    term = wt[:, i * count + r:i * count + r + 1] * part(r, base).astype(F32)
                    acc = term if acc is None else acc + term
                store(r, base, acc.astype(BF16))
            return carry

        lax.fori_loop(0, seqs // TILE, body, 0)

    def merge_core(k):
        got["c_l", k].wait_recv()
        got["c_o", k].wait_recv()
        weights, lam = mixing([own_l[k], r0_l[k]])
        for j in range(side):
            for h in range(2):
                m0_l[k, j, h] = lam[j * line + h * hrow:j * line + (h + 1) * hrow]
        turn(weights)
        slot = k % 2

        def store(r, base, value):
            m0_o[k, r // line, (r % line) // hrow, r % hrow, pl.ds(base, TILE), :] = value

        blend(half_rows,
              [lambda r, base: o_buf[slot, pl.ds(r * pitch + base, TILE), :],
               lambda r, base: r0_o[k, r, pl.ds(base, TILE), :]],
              store)
        far, next_, prev = wrap(a2 + 2), wrap(a2 + 1), wrap(a2 - 1)
        plan = [(far, 0, rel_o.at[k, 0], rel_l.at[k, 0], right),
                (far, 1, rel_o.at[k, 1], rel_l.at[k, 1], left),
                (next_, 1, frm_o.at[k, 0, 1], frm_l.at[k, 0, 1], right),
                (prev, 0, frm_o.at[k, 1, 0], frm_l.at[k, 1, 0], left)]
        for i, (j, h, dst_o, dst_l, to) in enumerate(plan):
            push(("2_l", k, i), m0_l.at[k, j, h], dst_l, rs2_s.at[k, i, 1], rs2_r.at[k, i, 1], to)
            push(("2_o", k, i), m0_o.at[k, j, h], dst_o, rs2_s.at[k, i, 0], rs2_r.at[k, i, 0], to)

    def relay(k):
        plan = [(wrap(a2 + 1), 0, right), (wrap(a2 - 1), 1, left)]
        for i, (j, h, to) in enumerate(plan):
            got["2_l", k, i].wait_recv()
            got["2_o", k, i].wait_recv()
            weights, lam = mixing([m0_l[k, j, h], rel_l[k, i]])
            com_l[k, i] = lam
            turn(weights)

            def store(r, base, value, i=i):
                com_o[k, i, r, pl.ds(base, TILE), :] = value

            blend(hrow,
                  [lambda r, base, j=j, h=h: m0_o[k, j, h, r, pl.ds(base, TILE), :],
                   lambda r, base, i=i: rel_o[k, i, r, pl.ds(base, TILE), :]],
                  store)
            push(("2_l", k, 4 + i), com_l.at[k, i], frm_l.at[k, i, i], rs2_s.at[k, 4 + i, 1], rs2_r.at[k, 4 + i, 1], to)
            push(("2_o", k, 4 + i), com_o.at[k, i], frm_o.at[k, i, i], rs2_s.at[k, 4 + i, 0], rs2_r.at[k, 4 + i, 0], to)

    def merge2(k):
        for i in range(2, 6):
            got["2_l", k, i].wait_recv()
            got["2_o", k, i].wait_recv()

        def whole(ref):
            return jnp.concatenate([ref[0], ref[1]], axis=0)

        weights, lam = mixing([whole(m0_l.at[k, a2]), whole(frm_l.at[k, 0]), whole(frm_l.at[k, 1])])
        for j in range(side):
            m1_l[k, j] = lam[j * own:(j + 1) * own]
        turn(weights)

        def store(r, base, value):
            m1_o[k, r // own, r % own, pl.ds(base, TILE), :] = value

        blend(line,
              [lambda r, base: m0_o[k, a2, r // hrow, r % hrow, pl.ds(base, TILE), :],
               lambda r, base: frm_o[k, 0, r // hrow, r % hrow, pl.ds(base, TILE), :],
               lambda r, base: frm_o[k, 1, r // hrow, r % hrow, pl.ds(base, TILE), :]],
              store)
        for i, dev in enumerate(peers):
            j = wrap(a1 + i + 1)
            push(("1_l", k, i), m1_l.at[k, j], r1_l.at[k, i], rs1_s.at[k, i, 1], rs1_r.at[k, i, 1], dev)
            push(("1_o", k, i), m1_o.at[k, j], r1_o.at[k, i], rs1_s.at[k, i, 0], rs1_r.at[k, i, 0], dev)

    def merge1(k):
        for i in range(side - 1):
            got["1_l", k, i].wait_recv()
            got["1_o", k, i].wait_recv()
        weights, _ = mixing([m1_l[k, a1]] + [r1_l[k, i] for i in range(side - 1)])
        turn(weights)

        def store(r, base, value):
            out_ref[r, pl.ds(k * seqs + base, TILE), :] = value

        blend(own,
              [lambda r, base: m1_o[k, a1, r, pl.ds(base, TILE), :]]
              + [lambda r, base, i=i: r1_o[k, i, r, pl.ds(base, TILE), :] for i in range(side - 1)],
              store)

    stages = {"g1": gather1, "g2": gather2, "g3": gather3, "g4": gather4, "g5": gather5,
              "at": attend, "mc": merge_core, "rl": relay, "m2": merge2, "m1": merge1}
    for name, k in order(chunks):
        stages[name](k)
    for copy in sent:
        copy.wait_send()


def order(chunks):
    plan = [("g1", k) for k in range(chunks)]
    ticks = []
    lag = {"g2": 0, "g3": 2, "g4": 3, "g5": 4, "at": 4, "mc": 5, "rl": 6, "m2": 7, "m1": 8}
    rank = {"g2": 2, "g3": 0, "g4": 1, "mc": 3, "rl": 4, "m2": 5, "m1": 6, "g5": 7, "at": 8}
    for k in range(chunks):
        for name, late in lag.items():
            ticks.append((k + late, rank[name], k, name))
    return plan + [(name, k) for _, _, k, name in sorted(ticks)]


def solution(mesh):
    dup_size = mesh.shape["dup"]
    side = math.isqrt(dup_size // CORES)
    chunks = 4

    def group_step(q_local, k_span, v_span, len_local):
        num_batch, span, head_dim = k_span.shape
        own = q_local.shape[1]
        rows = own * dup_size
        half_rows = rows // CORES
        line = side * own
        hrow = line // 2
        seqs = num_batch // chunks
        pitch = seqs + 8
        vm = pltpu.VMEM
        dma = pltpu.SemaphoreType.DMA
        out = pl.pallas_call(
            functools.partial(kernel, side, chunks, span),
            out_shape=jax.ShapeDtypeStruct((own, num_batch, head_dim), BF16),
            in_specs=[pl.BlockSpec(memory_space=pl.ANY)] * 3 + [pl.BlockSpec(memory_space=pltpu.SMEM)],
            out_specs=pl.BlockSpec(memory_space=pltpu.VMEM),
            scratch_shapes=[
                vm((num_batch, span, head_dim), BF16), vm((num_batch, span, head_dim), BF16),
                vm((chunks, seqs, CORES, side, side, own, head_dim), BF16),
                vm((2, rows * pitch, head_dim), F32), vm((LANES, LANES), F32),
                vm((chunks, half_rows, seqs, head_dim), BF16), vm((chunks, half_rows, LANES), F32),
                vm((chunks, half_rows, seqs, head_dim), BF16), vm((chunks, half_rows, LANES), F32),
                vm((chunks, half_rows, LANES), F32),
                vm((chunks, side, 2, hrow, seqs, head_dim), BF16), vm((chunks, side, 2, hrow, LANES), F32),
                vm((chunks, 2, hrow, seqs, head_dim), BF16), vm((chunks, 2, hrow, LANES), F32),
                vm((chunks, 2, hrow, seqs, head_dim), BF16), vm((chunks, 2, hrow, LANES), F32),
                vm((chunks, 2, 2, hrow, seqs, head_dim), BF16), vm((chunks, 2, 2, hrow, LANES), F32),
                vm((chunks, side, own, seqs, head_dim), BF16), vm((chunks, side, own, LANES), F32),
                vm((chunks, side - 1, own, seqs, head_dim), BF16), vm((chunks, side - 1, own, LANES), F32),
                dma((3, chunks)),
                dma((chunks, side - 1)), dma((chunks, side - 1)),
                dma((chunks, 4)), dma((chunks, 4)),
                dma((chunks, side)), dma((chunks, side)),
                dma((chunks, 2)), dma((chunks, 2)),
                dma((chunks, 6, 2)), dma((chunks, 6, 2)),
                dma((chunks, side - 1, 2)), dma((chunks, side - 1, 2)),
            ],
            compiler_params=pltpu.CompilerParams(
                collective_id=0, has_side_effects=True, vmem_limit_bytes=60 * 1024 * 1024),
            name="decode_group",
        )(q_local, k_span, v_span, len_local)
        return jnp.swapaxes(out, 0, 1)

    return jax.shard_map(group_step, mesh=mesh, in_specs=(P("kv", "dup", None), P("kv", "dup", None), P("kv", "dup", None), P("kv")), out_specs=P("kv", "dup", None), check_vma=False)
```

time: 181 us -> 124 us (0.69)
  Pallas kernels: 0 us -> 121 us
  waiting for transfers between devices: 96.9 us -> 0 us
  other arithmetic: 21.8 us -> 0 us
  matrix products: 21.4 us -> 0 us
  between operations: 13.5 us -> 0.01 us
  local copies, waits for them, and re-layouts: 14.7 us -> 1.7 us
  starting transfers between devices: 11 us -> 0 us
    pallas_call x0 -> x1, Pallas kernels: none -> 121 us  [group_step(): pl.pallas_call(functools.partial(kernel, side, chunks, span), out_shape=j...]
    all_to_all x2 -> x0, waiting for transfers between devices: 53 us -> none  [the longest x1 53 us: group_step(): recv_out = lax.all_to_all(part_out, 'dup', 1, 1)]
    all_gather x1 -> x0, waiting for transfers between devices: 43.9 us -> none  [group_step(): q_group = lax.all_gather(q_local, 'dup', axis=1, tiled=True)]
    dot_general x2 -> x0, matrix products: 21.4 us -> none  [the longest x1 11.1 us: group_step(): jnp.einsum('brs,bsd->brd', prob_vals.astype(jnp.bfloat16), v_span, prefer...]
    reduce_sum x3 -> x0, other arithmetic: 20 us -> none  [the longest x1 11.5 us: group_step(): merged = jnp.sum(weights[..., None] * recv_out.astype(jnp.float32), axis=1)]
    all_to_all x2 -> x0, starting transfers between devices: 11 us -> none  [the longest x1 6.33 us: group_step(): recv_out = lax.all_to_all(part_out, 'dup', 1, 1)]
    reshape x1 -> x0, local copies, waits for them, and re-layouts: 6.42 us -> none  [group_step(): (weighted / row_mass).astype(jnp.bfloat16)]
    unnamed x3 -> x0, local copies, waits for them, and re-layouts: 4.79 us -> none
  transfers between devices with their start and end apart: 3 -> 0, of which waited for: 2 -> 0; matrix products, arithmetic and copies ran while one was open for 12% -> 0% of each run, Pallas kernels for 0% -> 0%
where the time goes in v1:
time: 124 us; the launch traced here: 123 us
  Pallas kernels  121 us (98%)
  local copies, waits for them, and re-layouts  1.7 us (1%)
    pallas_call x1, Pallas kernels, group_step(): pl.pallas_call(functools.partial(kernel, side, chunks, span), out_shape=j...  121 us

profile of v1, /device:TPU:96, one launch (start us, length us, event | category | flops | bytes accessed | tf_op | source)
XLA Modules:
  0.0 122.9 jit_solution(9340674007188060275)
XLA Ops:
  0.0 121.2 %decode_group.1 = bf16[2,256,128]{2,1,0:T(8,128)(2,1)} custom-call(bf16[256,2,128]{2,1,0:T(2,128)(2,1)} %q_hbm.1, bf16[256,128,128]{2,1,0:T(8,128)(2,1)} %k_hbm.1, bf16[256,128,128]{2,1,0:T(8,128)(2,1)} %v_hbm.1, s32[256]{0:T(256)} %len_ref.1), custom_call_target="tpu_custom_call" | custom-call | tf_op jit(solution)/shard_map/decode_group/pallas_call | solution.py:315
  121.2 1.7 %copy.5 = bf16[256,2,128]{2,1,0:T(2,128)(2,1)} copy(bf16[256,2,128]{2,0,1:T(8,128)(2,1)} %bitcast.1) | data formatting | bytes 262144 | tf_op jit(solution)/shard_map/transpose | solution.py:345
